TPU v7x, 256 devices: a whole 4x4x8 slice. The times are simulated.
256 devices in a mesh: tok: 32 (over z_lo, x, core), blk: 8 (over y, z_hi).
Axes of the slice: x: 4, y: 4, z: 8 (z_hi: 2, z_lo: 4; z = z_hi * 4 + z_lo), core: 2. Of those that a mesh axis runs over, the one named last changes fastest.
Arguments:
- activations: bfloat16 [4096, 7168], P('tok', 'blk'), may hold values from -600 to 600
- signs: float32 [7168], P('blk'), may hold values from -1 to 1, as said below
Outputs:
- hessian: float32 [7168, 7168], P('tok', 'blk')
- incoherence: float32 [7168], P('blk')
- largest_ratio: float32 [], replicated
Inputs may be any that keep to these rules, and one draw needn't show every extreme that they name: `signs`: every entry is -1 or 1.
All inputs are finite; a program needn't handle non-finite values.
Results may differ from a plain program's by a relative error of at most 0.0037.
Values may be sent and summed in bfloat16 or wider, within the bound.
A program may use at most 128 MiB of HBM per device.

v0:
```python
import functools
import math

import jax
import jax.numpy as jnp
from jax import lax
from jax.sharding import Mesh
from jax.sharding import PartitionSpec as P

WALSH = 512
MIX = 14
FEATURES = 7168
BLK = ("blk_0", "blk_1")
TOK = ("tok_0", "tok_1", "tok_2")
TOK_BLK = ("tok_0", "tok_1", "tok_2", "blk_0", "blk_1")


EPS = 1e-06
DAMP = 0.01


def over_axes(value, axes):
    return functools.reduce(lax.psum, axes, value)


def laid_out(pieces, dim):
    pieces = jnp.moveaxis(pieces, 0, dim)
    dims = pieces.shape
    return pieces.reshape(*dims[:dim], dims[dim] * dims[dim + 1], *dims[dim + 2 :])


def from_everyone(value, axis):
    copies = jnp.broadcast_to(value, (lax.axis_size(axis), *value.shape))
    return lax.all_to_all(copies, axis, split_axis=0, concat_axis=0, tiled=True)


def gather_directly(value, axis, dim):
    return laid_out(from_everyone(value, axis), dim)


def over_copies(value, axis):
    everything = from_everyone(value, axis)
    return jnp.max(everything, axis=0)


def walsh_table(length):
    position = jnp.arange(length, dtype=jnp.int32)
    parity = jnp.zeros((length, length), jnp.int32)
    for bit_number in range(length.bit_length() - 1):
        parity = parity + (position[:, None] >> bit_number & 1) * (
            position[None, :] >> bit_number & 1
        )
    return (1 - 2 * (parity % 2)).astype(jnp.float32)


def cosine_table(length):
    rows_idx = jnp.arange(length, dtype=jnp.float32)[:, None]
    columns = jnp.arange(length, dtype=jnp.float32)[None, :]
    table = math.sqrt(2.0 / length) * jnp.cos(math.pi * (columns + 0.5) * rows_idx / length)
    return jnp.where(rows_idx == 0.0, table * math.sqrt(0.5), table)


def contract_tokens(left, right):
    return lax.dot_general(
        left, right, (((0,), (0,)), ((), ())), preferred_element_type=jnp.float32
    )


def per_device(activations, signs):
    tok_rows, block_width = activations.shape
    blocks = lax.axis_size(BLK)
    block_index = lax.axis_index(BLK)
    token_groups = lax.axis_size(TOK)
    token_index = lax.axis_index(TOK)
    local_walsh = WALSH // blocks
    signed = activations * signs.astype(jnp.bfloat16)[None, :]
    local_table = jnp.kron(walsh_table(local_walsh) / math.sqrt(local_walsh), cosine_table(MIX).T)
    partial_mix = jnp.dot(signed.astype(jnp.float32), local_table, precision=lax.Precision.HIGHEST)
    grouped = partial_mix.reshape(blocks, tok_rows // blocks, 1, block_width)
    cross_table = walsh_table(blocks) / math.sqrt(blocks)
    combined = jnp.einsum(
        "rs,xisf->xirf",
        cross_table,
        lax.all_to_all(grouped, BLK, split_axis=0, concat_axis=2, tiled=True),
        precision=lax.Precision.HIGHEST,
    )
    spread = lax.all_to_all(
        combined.astype(jnp.bfloat16), BLK, split_axis=2, concat_axis=0, tiled=True
    )
    rotated = spread.reshape(tok_rows, block_width)
    rotated_wide = rotated.astype(jnp.float32)
    trace_total = over_axes(jnp.sum(rotated_wide * rotated_wide), TOK_BLK)
    row_count = FEATURES // token_groups
    gathered = gather_directly(rotated, BLK, 1)
    gram_block = lax.psum_scatter(
        contract_tokens(gathered, rotated), TOK, scatter_dimension=0, tiled=True
    )
    global_rows = token_index * row_count + jnp.arange(row_count, dtype=jnp.int32)[:, None]
    global_columns = block_index * block_width + jnp.arange(block_width, dtype=jnp.int32)[None, :]
    on_diag = global_rows == global_columns
    local_peaks = jnp.max(jnp.where(on_diag, 0.0, jnp.abs(gram_block)), axis=0)
    column_peak = over_copies(local_peaks, TOK)
    diag_mean = trace_total / FEATURES + EPS
    hessian = gram_block / diag_mean + DAMP * on_diag.astype(jnp.float32)
    incoherence = column_peak / diag_mean
    largest_ratio = over_copies(jnp.max(incoherence), BLK)
    return (hessian, incoherence, largest_ratio)


def solution(mesh):
    split = Mesh(mesh.devices.reshape(4, 4, 2, 4, 2), ("tok_0", "tok_1", "tok_2", "blk_0", "blk_1"))
    return jax.shard_map(
        per_device,
        mesh=split,
        in_specs=(P(TOK, BLK), P(BLK)),
        out_specs=(P(TOK, BLK), P(BLK), P()),
        check_vma=False,
    )
```

profile of v0, /device:TPU:1, one launch (start us, length us, event | category | flops | bytes accessed | tf_op | source)
XLA Modules:
  0.0 367.2 jit_solution(6136312836264446147)
XLA Ops:
  7.5 13.5 %broadcast_multiply_fusion = f32[64,14,64,14]{3,2,1,0:T(8,128)} fusion(f32[14,14]{1,0:T(8,128)S(1)} %multiply_select_fusion, f32[64,64]{1,0:T(8,128)S(1)} %fusion.9), kind=kLoop, calls=%fused_computation | loop fusion | flops 802816 | bytes 3228432 | tf_op jit(solution)/shard_map/jit(kron)/mul | solution.py:77
  21.0 21.0 %reshape.408 = f32[896,896,1]{1,0,2:T(8,128)S(1)} reshape(f32[64,14,64,14]{3,2,1,0:T(8,128)} %broadcast_multiply_fusion) | data formatting | bytes 6422528 | tf_op jit(solution)/shard_map/jit(kron)/mul | solution.py:77
  42.0 2.2 convolution_bitcast_fusion
  44.2 11.6 %all-to-all-start = ((f32[8,16,1,896]{3,1,2,0:T(8,128)}), f32[8,16,1,896]{3,1,2,0:T(8,128)S(1)}, u32[]{:S(2)}, u32[]{:S(2)}) async-start(f32[8,16,1,896]{3,1,2,0:T(8,128)} %convolution_bitcast_fusion), calls=%async_computation | async-start | bytes 917504 | tf_op jit(solution)/shard_map/all_to_all | solution.py:84
  55.9 12.6 %all-to-all-done = f32[8,16,1,896]{3,1,2,0:T(8,128)S(1)} async-done(((f32[8,16,1,896]{3,1,2,0:T(8,128)}), f32[8,16,1,896]{3,1,2,0:T(8,128)S(1)}, u32[]{:S(2)}, u32[]{:S(2)}) %all-to-all-start) | async-done | bytes 458784 | tf_op jit(solution)/shard_map/all_to_all | solution.py:84
  68.5 0.6 fusion
  69.1 12.3 %all_to_all.47 = bf16[1,16,8,896]{3,1,0,2:T(8,128)(2,1)S(1)} all-to-all(bf16[1,16,8,896]{3,1,0,2:T(8,128)(2,1)S(1)} %copy.19), channel_id=1, replica_groups=mesh['tok_0'=4,'tok_1'=4,'tok_2'=2,'blk_0'=4,'blk_1'=2] {'blk_0','blk_1'}, dimensions={2} | all-to-all | bytes 458752 | tf_op jit(solution)/shard_map/all_to_all | solution.py:87
  81.4 0.2 copy.20
  81.6 0.2 broadcast_in_dim.15
  81.8 24.9 %all_to_all.48 = bf16[8,128,896]{1,2,0:T(8,128)(2,1)S(1)} all-to-all(bf16[8,128,896]{1,2,0:T(8,128)(2,1)S(1)} %broadcast_in_dim.15), channel_id=1, replica_groups=mesh['tok_0'=4,'tok_1'=4,'tok_2'=2,'blk_0'=4,'blk_1'=2] {'blk_0','blk_1'}, dimensions={0} | all-to-all | bytes 3670016 | tf_op jit(solution)/shard_map/all_to_all | solution.py:34
  106.7 10.3 %fusion.35 = f32[7168,896]{1,0:T(8,128)} fusion(bf16[128,7168]{0,1:T(8,128)(2,1)S(1)} %bitcast.34, bf16[128,896]{1,0:T(8,128)(2,1)S(1)} %bitcast.36), kind=kOutput, calls=%fused_computation.62 | convolution fusion | flops 1644167168 | bytes 27754496 | tf_op jit(solution)/shard_map/dot_general | solution.py:64
  117.0 0.7 multiply_reduce_fusion
  117.7 34.7 %psum.35 = f32[]{:T(128)} all-reduce(f32[]{:T(128)} %multiply_reduce_fusion), channel_id=1, replica_groups=mesh['tok_0'=4,'tok_1'=4,'tok_2'=2,'blk_0'=4,'blk_1'=2] {'tok_0'}, use_global_device_ids=true, to_apply=%region_2.3 | all-reduce | flops 1 | bytes 8 | tf_op jit(solution)/shard_map/psum | solution.py:23
  152.4 12.9 %psum.36 = f32[]{:T(128)} all-reduce(f32[]{:T(128)} %psum.35), channel_id=1, replica_groups=mesh['tok_0'=4,'tok_1'=4,'tok_2'=2,'blk_0'=4,'blk_1'=2] {'tok_1'}, use_global_device_ids=true, to_apply=%region_3.4 | all-reduce | flops 1 | bytes 8 | tf_op jit(solution)/shard_map/psum | solution.py:23
  165.4 3.8 %psum.37 = f32[]{:T(128)} all-reduce(f32[]{:T(128)} %psum.36), channel_id=1, replica_groups=mesh['tok_0'=4,'tok_1'=4,'tok_2'=2,'blk_0'=4,'blk_1'=2] {'tok_2'}, use_global_device_ids=true, to_apply=%region_4.5 | all-reduce | flops 1 | bytes 8 | tf_op jit(solution)/shard_map/psum | solution.py:23
  169.1 8.8 %psum.38 = f32[]{:T(128)} all-reduce(f32[]{:T(128)} %psum.37), channel_id=1, replica_groups=mesh['tok_0'=4,'tok_1'=4,'tok_2'=2,'blk_0'=4,'blk_1'=2] {'blk_0'}, use_global_device_ids=true, to_apply=%region_5.6 | all-reduce | flops 1 | bytes 8 | tf_op jit(solution)/shard_map/psum | solution.py:23
  178.0 8.7 %psum.39 = f32[]{:T(128)} all-reduce(f32[]{:T(128)} %psum.38), channel_id=1, replica_groups=mesh['tok_0'=4,'tok_1'=4,'tok_2'=2,'blk_0'=4,'blk_1'=2] {'blk_1'}, use_global_device_ids=true, to_apply=%region_6.7 | all-reduce | flops 1 | bytes 8 | tf_op jit(solution)/shard_map/psum | solution.py:23
  187.3 135.7 %reduce-scatter.2.cloned.1.call-done = f32[224,896]{1,0:T(8,128)} async-done(((f32[7168,896]{1,0:T(8,128)}), f32[224,896]{1,0:T(8,128)}) %reduce-scatter.2.cloned.1.call-update) | async-done | bytes 802832 | tf_op jit(solution)/shard_map/reduce_scatter | solution.py:95
  323.0 2.3 fusion.2
  325.3 16.7 %all_to_all.49 = f32[32,1,896]{2,1,0:T(1,128)S(1)} all-to-all(f32[32,1,896]{2,1,0:T(1,128)S(1)} %broadcast_in_dim.16), channel_id=1, replica_groups=mesh['tok_0'=4,'tok_1'=4,'tok_2'=2,'blk_0'=4,'blk_1'=2] {'tok_0','tok_1'..., dimensions={0} | all-to-all | bytes 229376 | tf_op jit(solution)/shard_map/all_to_all | solution.py:34
  342.1 1.2 fusion.34
  343.3 0.6 broadcast_in_dim.17
  343.9 15.8 %all_to_all.50 = f32[8,1,1]{2,1,0:T(1,128)S(1)} all-to-all(f32[8,1,1]{2,1,0:T(1,128)S(1)} %broadcast_in_dim.17), channel_id=1, replica_groups=mesh['tok_0'=4,'tok_1'=4,'tok_2'=2,'blk_0'=4,'blk_1'=2] {'blk_0','blk_1'}, dimensions={0} | all-to-all | bytes 64 | tf_op jit(solution)/shard_map/all_to_all | solution.py:34
  359.8 0.6 reduce_max.39
  (22 shorter events, 0.6 us)
Async XLA Ops:
  21.0 21.0 %copy-start.1 = (f32[896]{0:T(1024)S(1)}, f32[896]{0:T(1024)}, u32[]{:S(2)}) copy-start(f32[896]{0:T(1024)} %param.3) | copy-start | bytes 10756
  21.0 21.0 %copy-start = (bf16[128,896]{1,0:T(8,128)(2,1)S(1)}, bf16[128,896]{1,0:T(8,128)(2,1)}, u32[]{:S(2)}) copy-start(bf16[128,896]{1,0:T(8,128)(2,1)} %param.2) | copy-start | bytes 688132
  44.2 24.3 %all-to-all-start = ((f32[8,16,1,896]{3,1,2,0:T(8,128)}), f32[8,16,1,896]{3,1,2,0:T(8,128)S(1)}, u32[]{:S(2)}, u32[]{:S(2)}) async-start(f32[8,16,1,896]{3,1,2,0:T(8,128)} %convolution_bitcast_fusion), calls=%async_computation | async-start | bytes 917504 | tf_op jit(solution)/shard_map/all_to_all | solution.py:84
  55.8 267.1 %reduce-scatter.2.cloned.1.call-start = ((), (), s32[]{:S(2)}) async-start(), calls=%async_computation.6 | async-start | bytes 26492928 | tf_op jit(solution)/shard_map/reduce_scatter | solution.py:95
Sparse Core Ops, SparseCore 0:
  117.1 205.8 reduce-scatter.1
where the time goes:
time: 368 us; the launch traced here: 367 us
  waiting for transfers between devices  148 us (40%)
  blocking collectives  139 us (38%)
  local copies, waits for them, and re-layouts  22.1 us (6%)
  other arithmetic  18.7 us (5%)
  between operations  14.8 us (4%)
  matrix products  13.1 us (4%)
  starting transfers between devices  11.7 us (3%)
    reduce_scatter x1, waiting for transfers between devices, per_device(): lax.psum_scatter(contract_tokens(gathered, rotated), TOK, scatter_dimensi...  136 us
    psum x5, blocking collectives, over_axes(): return functools.reduce(lax.psum, axes, value)  69 us
    all_to_all x3, blocking collectives, from_everyone(): return lax.all_to_all(copies, axis, split_axis=0, concat_axis=0, tiled=True)  57.4 us
    mul x1, local copies, waits for them, and re-layouts, per_device(): jnp.kron(walsh_table(local_walsh) / math.sqrt(local_walsh), cosine_table(...  21 us
    mul x1, other arithmetic, per_device(): jnp.kron(walsh_table(local_walsh) / math.sqrt(local_walsh), cosine_table(...  13.5 us
    all_to_all x1, waiting for transfers between devices, per_device(): lax.all_to_all(grouped, BLK, split_axis=0, concat_axis=2, tiled=True)  12.6 us
    all_to_all x1, blocking collectives, per_device(): lax.all_to_all(combined.astype(jnp.bfloat16), BLK, split_axis=2, concat_a...  12.3 us
    all_to_all x1, starting transfers between devices, per_device(): lax.all_to_all(grouped, BLK, split_axis=0, concat_axis=2, tiled=True)  11.6 us
  transfers between devices with their start and end apart: 2, of which 2 were waited for; matrix products, arithmetic and copies ran while one was open for 0% of the time, Pallas kernels for 0%

commit v1 on v0

v1 whole, which is shorter than its diff:
```python
import math

import jax
import jax.numpy as jnp
import numpy as np
from jax import lax
from jax.sharding import PartitionSpec as P

WALSH = 512
MIX = 14
FEATURES = 7168
EPS = 1e-06
DAMP = 0.01


def walsh(length):
    table = np.ones((1, 1))
    while table.shape[0] < length:
        table = np.block([[table, table], [table, -table]])
    return table


def cosine(length):
    k = np.arange(length)[:, None]
    n = np.arange(length)[None, :]
    table = math.sqrt(2.0 / length) * np.cos(math.pi * (n + 0.5) * k / length)
    table[0] *= math.sqrt(0.5)
    return table


def split_table(local):
    table = np.kron(walsh(local), cosine(MIX).T) / math.sqrt(WALSH)
    high = table.astype(jnp.bfloat16)
    low = (table - high.astype(np.float64)).astype(jnp.bfloat16)
    return high, low


def contract_tokens(left, right):
    return lax.dot_general(left, right, (((0,), (0,)), ((), ())), preferred_element_type=jnp.float32)


def combine(parts):
    parts = list(parts)
    step = 1
    while step < len(parts):
        for i in range(0, len(parts), 2 * step):
            for j in range(i, i + step):
                parts[j], parts[j + step] = parts[j] + parts[j + step], parts[j] - parts[j + step]
        step *= 2
    return parts


def per_device(activations, signs):
    rows, width = activations.shape
    blocks = lax.axis_size("blk")
    toks = lax.axis_size("tok")
    b = lax.axis_index("blk")
    t = lax.axis_index("tok")
    share = rows // blocks
    row_count = FEATURES // toks
    high, low = split_table(WALSH // blocks)
    signed = activations * signs.astype(jnp.bfloat16)[None, :]
    mine = lax.all_to_all(signed.reshape(blocks, share, width), "blk", 0, 0, tiled=True)
    flat = mine.reshape(blocks * share, width)
    mixed = jnp.dot(flat, high, preferred_element_type=jnp.float32)
    mixed = mixed + jnp.dot(flat, low, preferred_element_type=jnp.float32)
    mixed = mixed.reshape(blocks, share, width)
    rotated = jnp.stack(combine([mixed[i] for i in range(blocks)])).astype(jnp.bfloat16)
    wide = rotated.astype(jnp.float32)
    trace_total = lax.psum(jnp.sum(wide * wide), ("tok", "blk"))
    columns = lax.all_to_all(rotated, "blk", 0, 0, tiled=True).reshape(rows, width)
    columns = lax.all_gather(columns, "tok", axis=0, tiled=True)
    pieces = jnp.moveaxis(rotated, 0, 1).reshape(share, toks, row_count)
    pieces = lax.all_to_all(jnp.moveaxis(pieces, 1, 0), "tok", 0, 0, tiled=True)
    pieces = lax.all_gather(pieces, "blk", axis=1, tiled=False)
    left = pieces.reshape(toks * rows, row_count)
    gram = contract_tokens(left, columns)
    at_rows = t * row_count + jnp.arange(row_count, dtype=jnp.int32)[:, None]
    at_columns = b * width + jnp.arange(width, dtype=jnp.int32)[None, :]
    on_diag = at_rows == at_columns
    peaks = jnp.max(jnp.where(on_diag, 0.0, jnp.abs(gram)), axis=0)
    peak = lax.pmax(peaks, "tok")
    largest = lax.pmax(jnp.max(peak), "blk")
    diag_mean = trace_total / FEATURES + EPS
    hessian = gram / diag_mean + DAMP * on_diag.astype(jnp.float32)
    return hessian, peak / diag_mean, largest / diag_mean


def solution(mesh):
    return jax.shard_map(
        per_device,
        mesh=mesh,
        in_specs=(P("tok", "blk"), P("blk")),
        out_specs=(P("tok", "blk"), P("blk"), P()),
        check_vma=False,
    )
```

time: 368 us -> 307 us (0.83); the launches traced: 367 us -> 302 us
  waiting for transfers between devices: 148 us -> 27 us
  blocking collectives: 139 us -> 241 us
  local copies, waits for them, and re-layouts: 22.1 us -> 5.32 us
  other arithmetic: 18.7 us -> 3.89 us
  starting transfers between devices: 11.7 us -> 0.08 us
  matrix products: 13.1 us -> 8.8 us
    reduce_scatter x1 -> x0, waiting for transfers between devices: 136 us -> none  [per_device(): lax.psum_scatter(contract_tokens(gathered, rotated), TOK, scatter_dimensi...]
    pmax x0 -> x2, blocking collectives: none -> 94.3 us  [the longest x1 67 us: per_device(): peak = lax.pmax(peaks, 'tok')]
    all_gather x0 -> x2, waiting for transfers between devices: none -> 27 us  [the longest x1 27 us: per_device(): columns = lax.all_gather(columns, 'tok', axis=0, tiled=True)]
    psum x5 -> x1, blocking collectives: 69 us -> 90.6 us  [per_device(): trace_total = lax.psum(jnp.sum(wide * wide), ('tok', 'blk'))]
    mul x1 -> x0, local copies, waits for them, and re-layouts: 21 us -> none  [per_device(): jnp.kron(walsh_table(local_walsh) / math.sqrt(local_walsh), cosine_table(...]
    all_to_all x4 -> x3, blocking collectives: 69.6 us -> 55.9 us  [the longest x1 21.4 us: per_device(): lax.all_to_all(signed.reshape(blocks, share, width), 'blk', 0, 0, tiled=T...]
    mul x2 -> x0, other arithmetic: 13.5 us -> none  [the longest x1 13.5 us: per_device(): jnp.kron(walsh_table(local_walsh) / math.sqrt(local_walsh), cosine_table(...]
    all_to_all x1 -> x0, waiting for transfers between devices: 12.6 us -> none  [per_device(): lax.all_to_all(grouped, BLK, split_axis=0, concat_axis=2, tiled=True)]
  transfers between devices with their start and end apart: 2 -> 2, of which waited for: 2 -> 1; matrix products, arithmetic and copies ran while one was open for 0% -> 2% of each run, Pallas kernels for 0% -> 0%
where the time goes in v1:
time: 307 us; the launch traced here: 302 us
  blocking collectives  241 us (79%)
  waiting for transfers between devices  27 us (9%)
  between operations  16.6 us (5%)
  matrix products  8.8 us (3%)
  local copies, waits for them, and re-layouts  5.32 us (2%)
  other arithmetic  3.89 us (1%)
    psum x1, blocking collectives, per_device(): trace_total = lax.psum(jnp.sum(wide * wide), ('tok', 'blk'))  90.6 us
    pmax x1, blocking collectives, per_device(): peak = lax.pmax(peaks, 'tok')  67 us
    pmax x1, blocking collectives, per_device(): largest = lax.pmax(jnp.max(peak), 'blk')  27.3 us
    all_gather x1, waiting for transfers between devices, per_device(): columns = lax.all_gather(columns, 'tok', axis=0, tiled=True)  27 us
    all_to_all x1, blocking collectives, per_device(): lax.all_to_all(signed.reshape(blocks, share, width), 'blk', 0, 0, tiled=T...  21.4 us
    all_to_all x1, blocking collectives, per_device(): pieces = lax.all_to_all(jnp.moveaxis(pieces, 1, 0), 'tok', 0, 0, tiled=True)  20.5 us
    all_to_all x1, blocking collectives, per_device(): lax.all_to_all(rotated, 'blk', 0, 0, tiled=True).reshape(rows, width)  14 us
    dot_general x1, matrix products, contract_tokens(): lax.dot_general(left, right, (((0,), (0,)), ((), ())), preferred_element_...  6.5 us
  transfers between devices with their start and end apart: 2, of which 1 were waited for; matrix products, arithmetic and copies ran while one was open for 2% of the time, Pallas kernels for 0%

profile of v1, /device:TPU:1, one launch (start us, length us, event | category | flops | bytes accessed | tf_op | source)
XLA Modules:
  0.0 302.4 jit_solution(10132613297484152521)
XLA Ops:
  7.2 0.0 copy-start
  7.2 0.0 all-gather.6.cloned.1.call-start
  7.2 0.8 convert_element_type.8
  8.0 1.0 broadcast_multiply_fusion
  9.0 21.4 %all_to_all.15 = bf16[8,16,896]{2,1,0:T(8,128)(2,1)S(1)} all-to-all(bf16[8,16,896]{2,1,0:T(8,128)(2,1)S(1)} %bitcast.56), channel_id=1, replica_groups=mesh['tok'=32,'blk'=8] {'blk'}, dimensions={0} | all-to-all | bytes 458752 | tf_op jit(solution)/shard_map/all_to_all | solution.py:63
  30.4 1.9 fusion.22
  32.3 0.4 convolution_add_fusion
  33.0 0.2 reshape.51
  33.2 0.2 copy.10
  33.4 20.5 %all_to_all.16 = bf16[32,16,224]{2,1,0:T(8,128)(2,1)S(1)} all-to-all(bf16[32,16,224]{2,1,0:T(8,128)(2,1)S(1)} %copy.10), channel_id=1, replica_groups=mesh['tok'=32,'blk'=8] {'tok'}, dimensions={0} | all-to-all | bytes 458752 | tf_op jit(solution)/shard_map/all_to_all | solution.py:74
  53.9 0.8 copy.11
  54.7 0.0 all-gather.6.cloned.1.call-update
  54.7 0.0 all-gather.4.cloned.1.call-start
  54.8 14.0 %all_to_all.17 = bf16[8,16,896]{2,1,0:T(8,128)(2,1)} all-to-all(bf16[8,16,896]{2,1,0:T(8,128)(2,1)S(1)} %fusion.20), channel_id=1, replica_groups=mesh['tok'=32,'blk'=8] {'blk'}, dimensions={0} | all-to-all | bytes 458752 | tf_op jit(solution)/shard_map/all_to_all | solution.py:71
  68.7 0.0 all-gather.4.cloned.1.call-update
  68.8 0.7 multiply_reduce_fusion
  69.5 90.6 %psum.7 = f32[]{:T(128)} all-reduce(f32[]{:T(128)} %multiply_reduce_fusion), channel_id=1, replica_groups=mesh['tok'=32,'blk'=8] {'tok','blk'}, use_global_device_ids=true, to_apply=%region_1.0 | all-reduce | flops 1 | bytes 8 | tf_op jit(solution)/shard_map/psum | solution.py:70
  160.7 0.0 all-gather.6.cloned.1.call-done
  160.8 4.1 %copy.12 = bf16[32,128,224]{1,0,2:T(8,128)(2,1)S(1)} copy(bf16[32,128,224]{2,0,1:T(8,128)(2,1)} %all-gather.6.cloned.1.call-done) | data formatting | bytes 3670016 | tf_op jit(solution)/shard_map/all_gather | solution.py:75
  164.8 27.0 %all-gather.4.cloned.1.call-done = bf16[4096,896]{1,0:T(8,128)(2,1)} async-done(((bf16[128,896]{1,0:T(8,128)(2,1)}), bf16[4096,896]{1,0:T(8,128)(2,1)}) %all-gather.4.cloned.1.call-update) | async-done | bytes 7340048 | tf_op jit(solution)/shard_map/all_gather | solution.py:72
  191.8 6.5 %fusion.4 = (f32[896]{0:T(1024)S(1)}, f32[224,896]{1,0:T(8,128)}) fusion(s32[896]{0:T(1024)S(1)} %iota_add_fusion, s32[224]{0:T(256)S(1)} %iota_add_fusion.1, f32[]{:T(128)S(6)} %add.82, bf16[4096,896]{1,0:T(8,128)(2,1)} %all-gather.4.cloned.1.call-done, bf16[28,8,32,128]{3,2,1,0:T(8,128)(2,1)S(1)} %bitcast.53), kind=kOutput, calls=%fused_computation.7 | convolution fusion | flops 1645571200 | bytes 9985924 | tf_op jit(solution)/shard_map/dot_general | solution.py:39
  198.3 67.0 %pmax.14 = f32[896]{0:T(1024)S(1)} all-reduce(f32[896]{0:T(1024)S(1)} %get-tuple-element.13), channel_id=1, replica_groups=mesh['tok'=32,'blk'=8] {'tok'}, use_global_device_ids=true, to_apply=%region_3.4 | all-reduce | flops 896 | bytes 7168 | tf_op jit(solution)/shard_map/pmax | solution.py:82
  265.3 1.2 fusion.21
  266.5 27.3 %pmax.15 = f32[]{:T(128)} all-reduce(f32[]{:T(128)} %get-tuple-element.15), channel_id=1, replica_groups=mesh['tok'=32,'blk'=8] {'blk'}, use_global_device_ids=true, to_apply=%region_5.6 | all-reduce | flops 1 | bytes 8 | tf_op jit(solution)/shard_map/pmax | solution.py:83
  (12 shorter events, 0.3 us)
Async XLA Ops:
  7.2 25.1 %copy-start = (bf16[896,896]{1,0:T(8,128)(2,1)S(1)}, bf16[896,896]{1,0:T(8,128)(2,1)}, u32[]{:S(2)}) copy-start(bf16[896,896]{1,0:T(8,128)(2,1)} %constant.30.clone) | copy-start | bytes 4816900
  7.2 153.6 %all-gather.6.cloned.1.call-start = ((), (), s32[]{:S(2)}) async-start(), calls=%async_computation.4 | async-start | bytes 2359296 | tf_op jit(solution)/shard_map/all_gather | solution.py:75
  54.7 137.1 %all-gather.4.cloned.1.call-start = ((), (), s32[]{:S(2)}) async-start(), calls=%async_computation.3 | async-start | bytes 7569408 | tf_op jit(solution)/shard_map/all_gather | solution.py:72
Sparse Core Ops, SparseCore 0:
  54.8 68.1 all-gather.5
  124.9 66.9 all-gather.3
